TPU v7x, 32 devices: a whole 2x2x4 slice. The times are simulated.
32 devices in a mesh: ctx: 16 (over z, x, core), head: 2 (over y).
Axes of the slice: x: 2, y: 2, z: 4, core: 2. Of those that a mesh axis runs over, the one named last changes fastest.
Arguments:
- queries: bfloat16 [8192, 4096], P('ctx', 'head'), may hold values from -10 to 10
- key_states: bfloat16 [8192, 1024], P('ctx', 'head'), may hold values from -10 to 10
- value_rows_stored: bfloat16 [8192, 1024], P('ctx', 'head'), may hold values from -6 to 6
- span_order: int32 [16, 4], replicated, may hold values from 0 to 3, each once within a row
- doc_lengths: int32 [16], replicated, may hold values from 1 to 1792, 8192 in all
- w_out: bfloat16 [4096, 4096], P('ctx', 'head'), may hold values from -0.09375 to 0.09375
Outputs:
- projected: bfloat16 [8192, 4096], P('ctx', 'head')
Inputs may be any that keep to these rules, and one draw needn't show every extreme that they name: `span_order`: each row is a permutation of 0 to 3, so each shard holds the 4 spans of its own 512 consecutive positions in some order. `doc_lengths`: the lengths sum to 8192; the longest is exactly 1792.
All inputs are finite; a program needn't handle non-finite values.
Results may differ from a plain program's by a relative error of at most 0.0055.
Values may be sent and summed in bfloat16 or wider, within the bound.
No kernel may reach another device: no remote copies, remote signals or barrier semaphores. Data moves between devices by JAX's collectives and lax.ppermute only.
A program may use at most 128 MiB of HBM per device.

v0:
```python
import math

import jax
import jax.numpy as jnp
from jax import lax
from jax.sharding import PartitionSpec as P

HEAD_SIZE = 128
BLK = 128
REACH = 4


def passed_along(array, axis, by):
    size = lax.axis_size(axis)
    pairs = [(i, i + by) for i in range(size) if 0 <= i + by < size]
    return lax.ppermute(array, axis, pairs)


def shard_positions(span_order, source, row_count):
    shard_count = span_order.shape[0]
    slot_order = lax.dynamic_index_in_dim(
        span_order, jnp.clip(source, 0, shard_count - 1), 0, keepdims=False
    )
    within = jnp.tile(jnp.arange(BLK, dtype=jnp.int32), row_count // BLK)
    return source * row_count + jnp.repeat(slot_order, BLK) * BLK + within


def documents(ends, positions):
    return jnp.sum((ends[None, :] <= positions[:, None]).astype(jnp.int32), axis=1)


def per_device(queries, key_states, value_rows_stored, span_order, doc_lengths, w_out):
    own_index = lax.axis_index("ctx")
    row_count = queries.shape[0]
    kv_heads = key_states.shape[1] // HEAD_SIZE
    queries_per_group = queries.shape[1] // key_states.shape[1]
    ends = jnp.cumsum(doc_lengths)
    key_parts = [key_states]
    value_parts = [value_rows_stored]
    position_parts = [shard_positions(span_order, own_index, row_count)]
    valid_parts = [jnp.ones((row_count,), jnp.bool_)]
    last_full = REACH
    carried = (key_states, value_rows_stored)
    for offset in range(1, last_full + 1):
        carried = passed_along((carried[0], carried[1]), "ctx", 1)
        source = own_index - offset
        key_parts.append(carried[0])
        value_parts.append(carried[1])
        position_parts.append(shard_positions(span_order, source, row_count))
        valid_parts.append(jnp.full((row_count,), source >= 0))
    all_keys = jnp.concatenate(key_parts, axis=0)
    all_values = jnp.concatenate(value_parts, axis=0)
    all_positions = jnp.concatenate(position_parts, axis=0)
    all_valid = jnp.concatenate(valid_parts, axis=0)
    all_docs = documents(ends, all_positions)
    tile_count = all_keys.shape[0] // BLK
    query_positions = position_parts[0]
    query_docs = documents(ends, query_positions)
    grouped = queries.reshape(row_count, kv_heads, queries_per_group, HEAD_SIZE)
    scale_factor = 1.0 / math.sqrt(HEAD_SIZE)

    def attend(carry, tile):
        tile_keys, tile_values, tile_positions, tile_docs, tile_valid = tile
        visible = (query_docs[:, None] == tile_docs[None, :]) & (
            tile_positions[None, :] <= query_positions[:, None]
        )
        visible = visible & tile_valid[None, :]

        def compute(state):
            running, totals, accum = state
            scores = jnp.einsum(
                "qhgd,khd->hgqk",
                grouped,
                tile_keys.reshape(BLK, kv_heads, HEAD_SIZE),
                preferred_element_type=jnp.float32,
            )
            masked = jnp.where(visible[None, None], scores * scale_factor, -1e30)
            newmax = jnp.maximum(running, jnp.max(masked, axis=-1))
            weights = jnp.where(visible[None, None], jnp.exp(masked - newmax[..., None]), 0.0)
            factor = jnp.exp(running - newmax)
            totals = totals * factor + jnp.sum(weights, axis=-1)
            update = jnp.einsum(
                "hgqk,khd->hgqd",
                weights.astype(jnp.bfloat16),
                tile_values.reshape(BLK, kv_heads, HEAD_SIZE),
                preferred_element_type=jnp.float32,
            )
            accum = accum * factor[..., None] + update
            return (newmax, totals, accum)

        return (lax.cond(jnp.any(visible), compute, lambda state: state, carry), None)

    initial = (
        jnp.full((kv_heads, queries_per_group, row_count), -1e30, jnp.float32),
        jnp.zeros((kv_heads, queries_per_group, row_count), jnp.float32),
        jnp.zeros((kv_heads, queries_per_group, row_count, HEAD_SIZE), jnp.float32),
    )
    tiles = (
        all_keys.reshape(tile_count, BLK, all_keys.shape[1]),
        all_values.reshape(tile_count, BLK, all_values.shape[1]),
        all_positions.reshape(tile_count, BLK),
        all_docs.reshape(tile_count, BLK),
        all_valid.reshape(tile_count, BLK),
    )
    final_state, unused = lax.scan(attend, initial, tiles)
    running, totals, accum = final_state
    attended = (
        (accum / totals[..., None])
        .transpose(2, 0, 1, 3)
        .reshape(row_count, queries.shape[1])
        .astype(jnp.bfloat16)
    )
    all_heads = lax.all_gather(attended, "head", axis=1, tiled=True)
    projected = jnp.dot(
        all_heads,
        lax.all_gather(w_out, "ctx", axis=0, tiled=True),
        preferred_element_type=jnp.float32,
    )
    return projected.astype(jnp.bfloat16)


def solution(mesh):
    placed = (P("ctx", "head"), P("ctx", "head"), P("ctx", "head"), P(), P(), P("ctx", "head"))
    return jax.shard_map(
        per_device, mesh=mesh, in_specs=placed, out_specs=P("ctx", "head"), check_vma=False
    )
```

profile of v0, /device:TPU:30, one launch (start us, length us, event | category | flops | bytes accessed | tf_op | source)
XLA Modules:
  0.0 442.7 jit_solution(10928415968826704750)
XLA Ops:
  6.5 1.9 collective-permute-start
  8.5 1.9 collective-permute-start.4
  10.4 1.1 add_reduce_fusion
  11.9 5.3 %collective-permute-done = bf16[512,512]{1,0:T(8,128)(2,1)S(1)} collective-permute-done((bf16[512,512]{1,0:T(8,128)(2,1)}, bf16[512,512]{1,0:T(8,128)(2,1)S(1)}, u32[]{:S(2)}, u32[]{:S(2)}) %collective-permute-start) | collective-permute-done | bytes 524320 | tf_op jit(solution)/shard_map/ppermute | solution.py:16
  17.2 1.9 collective-permute-start.1
  20.1 2.7 collective-permute-done.4
  22.9 1.9 collective-permute-start.5
  24.9 3.7 collective-permute-done.1
  28.6 1.9 collective-permute-start.2
  30.6 3.6 collective-permute-done.5
  34.2 1.9 collective-permute-start.6
  36.2 4.0 copy.29
  40.2 3.0 copy.31
  45.1 1.9 constant_dynamic-update-slice_fusion.4
  46.9 1.9 collective-permute-start.3
  48.9 1.9 constant_dynamic-update-slice_fusion.9
  50.7 1.9 collective-permute-start.7
  52.7 1.9 constant_dynamic-update-slice_fusion.3
  54.5 1.9 constant_dynamic-update-slice_fusion.8
  56.4 1.9 constant_dynamic-update-slice_fusion.2
  58.4 1.9 constant_dynamic-update-slice_fusion.7
  61.2 4.4 copy.30
  66.4 4.5 %copy.32 = bf16[20,128,512]{1,2,0:T(8,128)(2,1)} copy(bf16[20,128,512]{2,1,0:T(8,128)(2,1)} %bitcast.14) | data formatting | bytes 5242880
  70.9 2.4 broadcast_in_dim.79
  73.2 78.0 %while.15 = (s32[]{:T(128)}, f32[4,4,512]{2,1,0:T(4,128)S(1)}, f32[4,4,512]{2,1,0:T(4,128)S(1)}, f32[4,4,512,128]{3,2,1,0:T(8,128)}, s32[512]{0:T(512)S(1)}, /*i...) while((s32[]{:T(128)}, f32[4,4,512]{2,1,0:T(4,128)S(1)}, ...), condition=%wide.region_9.10_spmd.clone, body=%wide.region_3.9_spmd.clone.sunk | while | flops 552944128 | bytes 58205904 | solution.py:105
  74.8 7.8 %conditional.3 = ((f32[4,4,512]{2,1,0:T(4,128)S(1)}, f32[4,4,512]{2,1,0:T(4,128)S(1)}, f32[4,4,512,128]{3,2,1,0:T(8,128)})) conditional(s32[]{:T(128)} %convert_element_type.40, (f32[4,4,512]{2,1,0:T(4,128)S(1)}, f32[4,4,512]{2,1,0:T(4,128)S(1)}, f32[4,4,512,128]{3,2,1,0:T(8,128)}) %tuple.56, (pred[512,128]{0,1:T(8,128)(4,1)S(1)}, ...), branch_computations={%region_5.5_spmd, %region_6.8_spmd} | conditional | flops 552615936 | bytes 58130524 | solution.py:91
  78.0 2.7 multiply_add_fusion
  80.7 1.9 copy-done.1
  84.1 7.8 %conditional.3 = ((f32[4,4,512]{2,1,0:T(4,128)S(1)}, f32[4,4,512]{2,1,0:T(4,128)S(1)}, f32[4,4,512,128]{3,2,1,0:T(8,128)})) conditional(s32[]{:T(128)} %convert_element_type.40, (f32[4,4,512]{2,1,0:T(4,128)S(1)}, f32[4,4,512]{2,1,0:T(4,128)S(1)}, f32[4,4,512,128]{3,2,1,0:T(8,128)}) %tuple.56, (pred[512,128]{0,1:T(8,128)(4,1)S(1)}, ...), branch_computations={%region_5.5_spmd, %region_6.8_spmd} | conditional | flops 552615936 | bytes 58130524 | solution.py:91
  87.3 2.7 multiply_add_fusion
  90.0 1.9 copy-done.1
  93.4 7.8 %conditional.3 = ((f32[4,4,512]{2,1,0:T(4,128)S(1)}, f32[4,4,512]{2,1,0:T(4,128)S(1)}, f32[4,4,512,128]{3,2,1,0:T(8,128)})) conditional(s32[]{:T(128)} %convert_element_type.40, (f32[4,4,512]{2,1,0:T(4,128)S(1)}, f32[4,4,512]{2,1,0:T(4,128)S(1)}, f32[4,4,512,128]{3,2,1,0:T(8,128)}) %tuple.56, (pred[512,128]{0,1:T(8,128)(4,1)S(1)}, ...), branch_computations={%region_5.5_spmd, %region_6.8_spmd} | conditional | flops 552615936 | bytes 58130524 | solution.py:91
  96.6 2.7 multiply_add_fusion
  99.3 1.9 copy-done.1
  102.8 7.8 %conditional.3 = ((f32[4,4,512]{2,1,0:T(4,128)S(1)}, f32[4,4,512]{2,1,0:T(4,128)S(1)}, f32[4,4,512,128]{3,2,1,0:T(8,128)})) conditional(s32[]{:T(128)} %convert_element_type.40, (f32[4,4,512]{2,1,0:T(4,128)S(1)}, f32[4,4,512]{2,1,0:T(4,128)S(1)}, f32[4,4,512,128]{3,2,1,0:T(8,128)}) %tuple.56, (pred[512,128]{0,1:T(8,128)(4,1)S(1)}, ...), branch_computations={%region_5.5_spmd, %region_6.8_spmd} | conditional | flops 552615936 | bytes 58130524 | solution.py:91
  106.0 2.7 multiply_add_fusion
  108.6 1.9 copy-done.1
  112.1 7.8 %conditional.3 = ((f32[4,4,512]{2,1,0:T(4,128)S(1)}, f32[4,4,512]{2,1,0:T(4,128)S(1)}, f32[4,4,512,128]{3,2,1,0:T(8,128)})) conditional(s32[]{:T(128)} %convert_element_type.40, (f32[4,4,512]{2,1,0:T(4,128)S(1)}, f32[4,4,512]{2,1,0:T(4,128)S(1)}, f32[4,4,512,128]{3,2,1,0:T(8,128)}) %tuple.56, (pred[512,128]{0,1:T(8,128)(4,1)S(1)}, ...), branch_computations={%region_5.5_spmd, %region_6.8_spmd} | conditional | flops 552615936 | bytes 58130524 | solution.py:91
  115.3 2.7 multiply_add_fusion
  118.0 1.9 copy-done.1
  124.6 7.8 %conditional.3 = ((f32[4,4,512]{2,1,0:T(4,128)S(1)}, f32[4,4,512]{2,1,0:T(4,128)S(1)}, f32[4,4,512,128]{3,2,1,0:T(8,128)})) conditional(s32[]{:T(128)} %convert_element_type.40, (f32[4,4,512]{2,1,0:T(4,128)S(1)}, f32[4,4,512]{2,1,0:T(4,128)S(1)}, f32[4,4,512,128]{3,2,1,0:T(8,128)}) %tuple.56, (pred[512,128]{0,1:T(8,128)(4,1)S(1)}, ...), branch_computations={%region_5.5_spmd, %region_6.8_spmd} | conditional | flops 552615936 | bytes 58130524 | solution.py:91
  127.8 2.7 multiply_add_fusion
  130.4 1.9 copy-done.1
  151.2 5.2 %copy.33 = f32[4,4,512,128]{2,3,1,0:T(8,128)} copy(f32[4,4,512,128]{3,2,1,0:T(8,128)} %get-tuple-element.144) | data formatting | bytes 8388608 | tf_op jit(solution)/shard_map/while | solution.py:105
  156.5 4.1 divide_convert_fusion
  161.4 133.3 %all-gather.3.cloned.1.call-done = bf16[512,4096]{0,1:T(8,128)(2,1)} async-done(((bf16[512,2048]{0,1:T(8,128)(2,1)}), bf16[512,4096]{0,1:T(8,128)(2,1)}) %all-gather.3.cloned.1.call-update) | async-done | bytes 4194320 | tf_op jit(solution)/shard_map/all_gather | solution.py:113
  294.6 126.7 %all-gather.5.cloned.1.call-done = bf16[4096,2048]{1,0:T(8,128)(2,1)} async-done(((bf16[256,2048]{1,0:T(8,128)(2,1)}), bf16[4096,2048]{1,0:T(8,128)(2,1)}) %all-gather.5.cloned.1.call-update) | async-done | bytes 16777232 | tf_op jit(solution)/shard_map/all_gather | solution.py:116
  421.3 14.6 %convolution_convert_fusion = bf16[512,2048]{1,0:T(8,128)(2,1)} fusion(bf16[512,4096]{0,1:T(8,128)(2,1)} %all-gather.3.cloned.1.call-done, bf16[4096,2048]{1,0:T(8,128)(2,1)} %all-gather.5.cloned.1.call-done), kind=kOutput, calls=%fused_computation.27 | convolution fusion | flops 8590983168 | bytes 23068672 | tf_op jit(solution)/shard_map/dot_general | solution.py:114
  (191 shorter events, 42.6 us)
Async XLA Ops:
  6.5 288.1 %all-gather.3.cloned.1.call-start = ((), (), s32[]{:S(2)}) async-start(), calls=%async_computation | async-start | bytes 6291456 | tf_op jit(solution)/shard_map/all_gather | solution.py:113
  6.5 10.7 %collective-permute-start = (bf16[512,512]{1,0:T(8,128)(2,1)}, bf16[512,512]{1,0:T(8,128)(2,1)S(1)}, u32[]{:S(2)}, u32[]{:S(2)}) collective-permute-start(bf16[512,512]{1,0:T(8,128)(2,1)} %param.11), channel_id=1, source_target_pairs={{0,2},{2,4},{4,6},{6,8},{8,10},{10,12},{12,14},{14,16},{16,18},{18... | collective-permute-start | bytes 1572872 | tf_op jit(solution)/shard_map/ppermute | solution.py:16
  8.5 14.4 %collective-permute-start.4 = (bf16[512,512]{1,0:T(8,128)(2,1)}, bf16[512,512]{1,0:T(8,128)(2,1)S(1)}, u32[]{:S(2)}, u32[]{:S(2)}) collective-permute-start(bf16[512,512]{1,0:T(8,128)(2,1)} %param.12), channel_id=1, source_target_pairs={{0,2},{2,4},{4,6},{6,8},{8,10},{10,12},{12,14},{14,16},{16,18},{18... | collective-permute-start | bytes 1572872 | tf_op jit(solution)/shard_map/ppermute | solution.py:16
  17.2 23.0 %copy-start.5 = (bf16[512,512]{1,0:T(8,128)(2,1)}, bf16[512,512]{1,0:T(8,128)(2,1)S(1)}, u32[]{:S(2)}) copy-start(bf16[512,512]{1,0:T(8,128)(2,1)S(1)} %collective-permute-done) | copy-start | bytes 1572868
  17.2 11.3 %collective-permute-start.1 = (bf16[512,512]{1,0:T(8,128)(2,1)S(1)}, bf16[512,512]{1,0:T(8,128)(2,1)}, u32[]{:S(2)}, u32[]{:S(2)}) collective-permute-start(bf16[512,512]{1,0:T(8,128)(2,1)S(1)} %collective-permute-done), channel_id=1, source_target_pairs={{0,2},{2,4},{4,6},{6,8},{8,10},{10,12},{12,14},{14,16},{16,18},{18... | collective-permute-start | bytes 1572872 | tf_op jit(solution)/shard_map/ppermute | solution.py:16
  22.9 17.4 %copy-start.4 = (bf16[512,512]{1,0:T(8,128)(2,1)}, bf16[512,512]{1,0:T(8,128)(2,1)S(1)}, u32[]{:S(2)}) copy-start(bf16[512,512]{1,0:T(8,128)(2,1)S(1)} %collective-permute-done.4) | copy-start | bytes 1572868
  22.9 11.3 %collective-permute-start.5 = (bf16[512,512]{1,0:T(8,128)(2,1)S(1)}, bf16[512,512]{1,0:T(8,128)(2,1)}, u32[]{:S(2)}, u32[]{:S(2)}) collective-permute-start(bf16[512,512]{1,0:T(8,128)(2,1)S(1)} %collective-permute-done.4), channel_id=1, source_target_pairs={{0,2},{2,4},{4,6},{6,8},{8,10},{10,12},{12,14},{14,16},{16,18},{18... | collective-permute-start | bytes 1572872 | tf_op jit(solution)/shard_map/ppermute | solution.py:16
  28.6 18.4 %collective-permute-start.2 = (bf16[512,512]{1,0:T(8,128)(2,1)}, bf16[512,512]{1,0:T(8,128)(2,1)}, u32[]{:S(2)}, u32[]{:S(2)}) collective-permute-start(bf16[512,512]{1,0:T(8,128)(2,1)} %collective-permute-done.1), channel_id=1, source_target_pairs={{0,2},{2,4},{4,6},{6,8},{8,10},{10,12},{12,14},{14,16},{16,18},{18... | collective-permute-start | bytes 1572872 | tf_op jit(solution)/shard_map/ppermute | solution.py:16
  34.2 16.5 %collective-permute-start.6 = (bf16[512,512]{1,0:T(8,128)(2,1)}, bf16[512,512]{1,0:T(8,128)(2,1)}, u32[]{:S(2)}, u32[]{:S(2)}) collective-permute-start(bf16[512,512]{1,0:T(8,128)(2,1)} %collective-permute-done.5), channel_id=1, source_target_pairs={{0,2},{2,4},{4,6},{6,8},{8,10},{10,12},{12,14},{14,16},{16,18},{18... | collective-permute-start | bytes 1572872 | tf_op jit(solution)/shard_map/ppermute | solution.py:16
  36.2 7.2 %copy-start.2 = (bf16[512,512]{1,0:T(8,128)(2,1)S(1)}, bf16[512,512]{1,0:T(8,128)(2,1)}, u32[]{:S(2)}) copy-start(bf16[512,512]{1,0:T(8,128)(2,1)} %param.11) | copy-start | bytes 1572868
  36.2 8.0 %copy-start.3 = (bf16[512,512]{1,0:T(8,128)(2,1)S(1)}, bf16[512,512]{1,0:T(8,128)(2,1)}, u32[]{:S(2)}) copy-start(bf16[512,512]{1,0:T(8,128)(2,1)} %param.12) | copy-start | bytes 1572868
  46.9 13.3 %collective-permute-start.3 = (bf16[512,512]{1,0:T(8,128)(2,1)}, bf16[512,512]{1,0:T(8,128)(2,1)S(1)}, u32[]{:S(2)}, u32[]{:S(2)}) collective-permute-start(bf16[512,512]{1,0:T(8,128)(2,1)} %collective-permute-done.2), channel_id=1, source_target_pairs={{0,2},{2,4},{4,6},{6,8},{8,10},{10,12},{12,14},{14,16},{16,18},{18... | collective-permute-start | bytes 1572872 | tf_op jit(solution)/shard_map/ppermute | solution.py:16
  50.7 14.8 %collective-permute-start.7 = (bf16[512,512]{1,0:T(8,128)(2,1)}, bf16[512,512]{1,0:T(8,128)(2,1)S(1)}, u32[]{:S(2)}, u32[]{:S(2)}) collective-permute-start(bf16[512,512]{1,0:T(8,128)(2,1)} %collective-permute-done.6), channel_id=1, source_target_pairs={{0,2},{2,4},{4,6},{6,8},{8,10},{10,12},{12,14},{14,16},{16,18},{18... | collective-permute-start | bytes 1572872 | tf_op jit(solution)/shard_map/ppermute | solution.py:16
  75.8 2.2 copy-start
  80.7 1.9 copy-start.1
  85.1 2.2 copy-start
  90.0 1.9 copy-start.1
  94.5 2.2 copy-start
  99.3 1.9 copy-start.1
  103.8 2.2 copy-start
  108.6 1.9 copy-start.1
  113.1 2.2 copy-start
  118.0 1.9 copy-start.1
  125.6 2.2 copy-start
  130.4 1.9 copy-start.1
  160.6 260.7 %all-gather.5.cloned.1.call-start = ((), (), s32[]{:S(2)}) async-start(), calls=%async_computation.1 | async-start | bytes 17825792 | tf_op jit(solution)/shard_map/all_gather | solution.py:116
Sparse Core Ops, SparseCore 0:
  160.7 133.8 all-gather.2
  296.8 124.4 all-gather.4
where the time goes:
time: 450 us; the launch traced here: 443 us
  waiting for transfers between devices  276 us (61%)
  local copies, waits for them, and re-layouts  57.8 us (13%)
  matrix products  36.2 us (8%)
  other arithmetic  29.7 us (7%)
  starting transfers between devices  15.3 us (3%)
  loops' own time  14.2 us (3%)
  between operations  13.6 us (3%)
    all_gather x1, waiting for transfers between devices, per_device(): all_heads = lax.all_gather(attended, 'head', axis=1, tiled=True)  133 us
    all_gather x1, waiting for transfers between devices, per_device(): lax.all_gather(w_out, 'ctx', axis=0, tiled=True)  127 us
    unnamed x20, local copies, waits for them, and re-layouts  28.9 us
    dot_general x6, matrix products, compute(): jnp.einsum('hgqk,khd->hgqd', weights.astype(jnp.bfloat16), tile_values.re...  15.9 us
    reduce_or x20, other arithmetic, attend(): jnp.any(visible)  15.4 us
    ppermute x8, waiting for transfers between devices, passed_along(): return lax.ppermute(array, axis, pairs)  15.3 us
    ppermute x8, starting transfers between devices, passed_along(): return lax.ppermute(array, axis, pairs)  15.3 us
    dot_general x1, matrix products, per_device(): jnp.dot(all_heads, lax.all_gather(w_out, 'ctx', axis=0, tiled=True), pref...  14.6 us
  transfers between devices with their start and end apart: 10, of which 6 were waited for; matrix products, arithmetic and copies ran while one was open for 6% of the time, Pallas kernels for 0%

commit v1 on v0

v1 whole, which is shorter than its diff:
```python
import functools
import math

import jax
import jax.numpy as jnp
from jax import lax
from jax.experimental import pallas as pl
from jax.experimental.pallas import tpu as pltpu
from jax.sharding import PartitionSpec as P

HEAD_SIZE = 128
BLK = 128
FAR = 1 << 30
NEG = -1e30


def attend_kernel(
    heads, group, slots, table, queries, low_minus_lane, *refs
):
    buffers = refs[: slots // 4]
    out, held, stacked, scores, peak, total, accum, picked, picked_pos, sems = refs[slots // 4 :]
    rows = group * BLK
    copies = []
    for index, buffer in enumerate(buffers):
        span = buffer.shape[0]
        copies.append(
            pltpu.make_async_copy(buffer, held.at[pl.ds(index * span, span)], sems.at[index])
        )
        copies[-1].start()
    for copy in copies:
        copy.wait()
    constant = math.log2(math.e) / math.sqrt(HEAD_SIZE)
    lane = lax.broadcasted_iota(jnp.int32, (BLK, BLK), 1)
    row = lax.broadcasted_iota(jnp.int32, (BLK, BLK), 0)

    @pl.loop(0, queries.shape[0] // BLK)
    def per_block(block):
        q_pos = table[slots + block]
        low_first = table[slots + 4 + block]
        low_last = table[slots + 8 + block]
        q_rows = pl.ds(pl.multiple_of(block * BLK, BLK), BLK)

        def look(slot, count):
            k_pos = table[slot]
            picked[count] = slot
            picked_pos[count] = k_pos
            live = (k_pos <= q_pos) & (k_pos + (BLK - 1) >= low_first)
            return count + live.astype(jnp.int32)

        count = lax.fori_loop(0, slots, look, 0)
        picked[count] = 0
        picked_pos[count] = FAR
        pairs = (count + 1) // 2
        for h in range(heads):
            for j in range(group):
                col = (h * group + j) * HEAD_SIZE
                stacked[h, j * BLK : (j + 1) * BLK, :] = queries[q_rows, col : col + HEAD_SIZE]
            peak[h] = jnp.full((rows, BLK), NEG, jnp.float32)
            total[h] = jnp.zeros((rows, BLK), jnp.float32)
            accum[h] = jnp.zeros((rows, HEAD_SIZE), jnp.float32)
        upper = q_pos + row - lane
        lower = low_minus_lane[q_rows, :]

        def two(pair, col):
            first = pl.ds(pl.multiple_of(picked[2 * pair] * BLK, BLK), BLK)
            second = pl.ds(pl.multiple_of(picked[2 * pair + 1] * BLK, BLK), BLK)
            cols = slice(col, col + HEAD_SIZE)
            return jnp.concatenate([held[first, cols], held[second, cols]], axis=0)

        def products(pair, h):
            return lax.dot_general(
                stacked[h],
                two(pair, h * HEAD_SIZE),
                (((1,), (1,)), ((), ())),
                preferred_element_type=jnp.float32,
            )

        @pl.loop(0, pairs)
        def score(pair):
            pos_a = picked_pos[2 * pair]
            pos_b = picked_pos[2 * pair + 1]
            whole = (
                (pos_a + BLK <= q_pos + 1)
                & (pos_b + BLK <= q_pos + 1)
                & (pos_a >= low_last)
                & (pos_b >= low_last)
            )

            @pl.when(whole)
            def _():
                for h in range(heads):
                    value = products(pair, h)
                    scores[pair, h] = value
                    peak[h] = jnp.maximum(
                        peak[h], jnp.maximum(value[:, :BLK], value[:, BLK:])
                    )

            @pl.when(jnp.logical_not(whole))
            def _():
                seen_a = (upper >= pos_a) & (lower <= pos_a)
                seen_b = (upper >= pos_b) & (lower <= pos_b)
                for h in range(heads):
                    value = products(pair, h)
                    for j in range(group):
                        part = slice(j * BLK, (j + 1) * BLK)
                        left = jnp.where(seen_a, value[part, :BLK], NEG)
                        right = jnp.where(seen_b, value[part, BLK:], NEG)
                        scores[pair, h, part, :BLK] = left
                        scores[pair, h, part, BLK:] = right
                        peak[h, part, :] = jnp.maximum(
                            peak[h, part, :], jnp.maximum(left, right)
                        )

        for h in range(heads):
            top = jnp.max(peak[h], axis=1, keepdims=True) * constant
            peak[h] = jnp.broadcast_to(top, (rows, BLK))

        @pl.loop(0, pairs)
        def weigh(pair):
            for h in range(heads):
                top = peak[h]
                left = jnp.exp2(scores[pair, h, :, :BLK] * constant - top)
                right = jnp.exp2(scores[pair, h, :, BLK:] * constant - top)
                total[h] += left + right
                weights = jnp.concatenate([left, right], axis=1).astype(jnp.bfloat16)
                accum[h] += jnp.dot(
                    weights,
                    two(pair, (heads + h) * HEAD_SIZE),
                    preferred_element_type=jnp.float32,
                )

        for h in range(heads):
            inverse = 1.0 / jnp.sum(total[h], axis=1, keepdims=True)
            result = (accum[h] * inverse).astype(jnp.bfloat16)
            for j in range(group):
                col = (h * group + j) * HEAD_SIZE
                out[q_rows, col : col + HEAD_SIZE] = result[j * BLK : (j + 1) * BLK, :]


def attend(table, queries, part, parts, low_minus_lane, buffers):
    rows, width = queries.shape
    width //= parts
    heads = buffers[0].shape[1] // (2 * HEAD_SIZE)
    group = width // (heads * HEAD_SIZE)
    slots = 4 * len(buffers)
    whole = pl.BlockSpec(memory_space=pl.ANY)
    stack = group * BLK
    return pl.pallas_call(
        functools.partial(attend_kernel, heads, group, slots),
        out_shape=jax.ShapeDtypeStruct((rows, width), jnp.bfloat16),
        grid_spec=pltpu.PrefetchScalarGridSpec(
            num_scalar_prefetch=1,
            grid=(1,),
            in_specs=[
                pl.BlockSpec((rows, width), lambda i, t: (0, part)),
                pl.BlockSpec((rows, BLK), lambda i, t: (0, 0)),
            ]
            + [whole] * len(buffers),
            out_specs=pl.BlockSpec((rows, width), lambda i, t: (0, 0)),
            scratch_shapes=[
                pltpu.VMEM((slots * BLK, buffers[0].shape[1]), jnp.bfloat16),
                pltpu.VMEM((heads, stack, HEAD_SIZE), jnp.bfloat16),
                pltpu.VMEM((slots // 2, heads, stack, 2 * BLK), jnp.float32),
                pltpu.VMEM((heads, stack, BLK), jnp.float32),
                pltpu.VMEM((heads, stack, BLK), jnp.float32),
                pltpu.VMEM((heads, stack, HEAD_SIZE), jnp.float32),
                pltpu.SMEM((slots + 2,), jnp.int32),
                pltpu.SMEM((slots + 2,), jnp.int32),
                pltpu.SemaphoreType.DMA((len(buffers),)),
            ],
        ),
        cost_estimate=pl.CostEstimate(
            flops=4 * rows * width * 4 * rows, bytes_accessed=rows * width * 12, transcendentals=0
        ),
        name="attend",
    )(table, queries, low_minus_lane, *buffers)


def moved(array, axis, pairs):
    return lax.ppermute(array, axis, pairs)


def per_device(queries, key_states, value_rows_stored, span_order, doc_lengths, w_out):
    me = lax.axis_index("ctx")
    size = lax.axis_size("ctx")
    rows = queries.shape[0]
    kv_width = key_states.shape[1]
    parts = 2
    half = kv_width // parts
    layer = 4
    up = [(i, i + layer) for i in range(size - layer)]
    across = [(i, i ^ 2) for i in range(size)]
    partner = [(i, i ^ 1) for i in range(size)]
    is_right = (me // 2) % 2 == 1

    own = [
        jnp.concatenate(
            [key_states[:, p * half : (p + 1) * half], value_rows_stored[:, p * half : (p + 1) * half]],
            axis=1,
        )
        for p in range(parts)
    ]
    held = []
    for p in range(parts):
        own_p = moved(own[p], "ctx", partner)
        lower = moved(own[p], "ctx", up)
        side = moved(jnp.where(is_right, lower, own[p]), "ctx", across)
        held.append(
            [own[p], own_p, lower, moved(lower, "ctx", partner), side, moved(side, "ctx", partner)]
        )
    other = me ^ 1
    shards = jnp.stack([me, other, me - layer, other - layer, me - 2, other - 2])
    order = span_order[jnp.clip(shards, 0, size - 1)]
    spans = shards[:, None] * rows + order * BLK
    spans = jnp.where(shards[:, None] >= 0, spans, FAR).reshape(-1)
    ends = jnp.cumsum(doc_lengths)
    starts = ends - doc_lengths
    q_spans = spans[:4]

    def low(positions):
        at = positions[..., None]
        return jnp.max(jnp.where(starts <= at, starts, 0), axis=-1)

    table = jnp.concatenate([spans, q_spans, low(q_spans), low(q_spans + BLK - 1)]).astype(jnp.int32)
    q_pos = (q_spans[:, None] + jnp.arange(BLK, dtype=jnp.int32)).reshape(-1)
    low_minus_lane = low(q_pos)[:, None] - jnp.arange(BLK, dtype=jnp.int32)
    attended = []
    for p in range(parts):
        attended.append(attend(table, queries, p, parts, low_minus_lane, held[p]))
    all_w = lax.all_gather(w_out, "ctx", axis=0, tiled=True)
    mine = jnp.concatenate(attended, axis=1)
    theirs = jnp.concatenate([moved(a, "head", [(0, 1), (1, 0)]) for a in attended], axis=1)
    here = lax.axis_index("head")
    first = jnp.where(here == 0, mine, theirs)
    second = jnp.where(here == 0, theirs, mine)
    all_heads = jnp.concatenate([first, second], axis=1)
    projected = jnp.dot(all_heads, all_w, preferred_element_type=jnp.float32)
    return projected.astype(jnp.bfloat16)


def solution(mesh):
    placed = (P("ctx", "head"), P("ctx", "head"), P("ctx", "head"), P(), P(), P("ctx", "head"))
    return jax.shard_map(
        per_device, mesh=mesh, in_specs=placed, out_specs=P("ctx", "head"), check_vma=False
    )
```

time: 450 us -> 191 us (0.42); the launches traced: 443 us -> 189 us
  waiting for transfers between devices: 276 us -> 110 us
  local copies, waits for them, and re-layouts: 57.8 us -> 2.46 us
  Pallas kernels: 0 us -> 35.4 us
  other arithmetic: 29.7 us -> 5.56 us
  matrix products: 36.2 us -> 13.9 us
  loops' own time: 14.2 us -> 0 us
  starting transfers between devices: 15.3 us -> 7.98 us
    all_gather x2 -> x1, waiting for transfers between devices: 260 us -> 0.01 us  [per_device(): all_w = lax.all_gather(w_out, 'ctx', axis=0, tiled=True)]
    ppermute x8 -> x12, waiting for transfers between devices: 15.3 us -> 109 us  [moved(): return lax.ppermute(array, axis, pairs)]
    pallas_call x0 -> x2, Pallas kernels: none -> 35.4 us  [attend(): pl.pallas_call(functools.partial(attend_kernel, heads, group, slots), out...]
    unnamed x20, local copies, waits for them, and re-layouts: 28.9 us -> 0.21 us
    dot_general x13 -> x1, matrix products: 36.2 us -> 13.9 us  [per_device(): projected = jnp.dot(all_heads, all_w, preferred_element_type=jnp.float32)]
    reduce_or x20 -> x0, other arithmetic: 15.4 us -> none  [attend(): jnp.any(visible)]
    another operation x21 -> x0, loops' own time: 14.2 us -> none  [the longest x1 13.6 us: per_device(): final_state, unused = lax.scan(attend, initial, tiles)]
    cond x30 -> x0, local copies, waits for them, and re-layouts: 12.2 us -> none
  transfers between devices with their start and end apart: 10 -> 13, of which waited for: 6 -> 5; matrix products, arithmetic and copies ran while one was open for 6% -> 4% of each run, Pallas kernels for 0% -> 19%
where the time goes in v1:
time: 191 us; the launch traced here: 189 us
  waiting for transfers between devices  110 us (58%)
  Pallas kernels  35.4 us (19%)
  matrix products  13.9 us (7%)
  between operations  13.6 us (7%)
  starting transfers between devices  7.98 us (4%)
  other arithmetic  5.56 us (3%)
  local copies, waits for them, and re-layouts  2.46 us (1%)
    ppermute x12, waiting for transfers between devices, moved(): return lax.ppermute(array, axis, pairs)  109 us
    pallas_call x2, Pallas kernels, attend(): pl.pallas_call(functools.partial(attend_kernel, heads, group, slots), out...  35.4 us
    dot_general x1, matrix products, per_device(): projected = jnp.dot(all_heads, all_w, preferred_element_type=jnp.float32)  13.9 us
    ppermute x12, starting transfers between devices, moved(): return lax.ppermute(array, axis, pairs)  7.97 us
  transfers between devices with their start and end apart: 13, of which 5 were waited for; matrix products, arithmetic and copies ran while one was open for 4% of the time, Pallas kernels for 19%

profile of v1, /device:TPU:30, one launch (start us, length us, event | category | flops | bytes accessed | tf_op | source)
XLA Modules:
  0.0 189.0 jit_solution(7247913309386464218)
XLA Ops:
  6.5 0.7 all-gather.2.cloned.1.call-update
  7.3 1.3 fusion.9
  8.5 0.0 copy-start.7
  8.6 1.3 collective-permute-start.6
  9.9 0.1 collective-permute-start.5
  10.0 1.3 collective-permute-start.1
  11.3 0.6 collective-permute-start
  11.9 0.1 copy.11
  12.0 0.1 stack.41
  12.1 0.1 stack.48
  12.2 0.6 gather_fusion
  12.8 0.1 add_select_fusion
  12.8 53.6 %collective-permute-done.1.refs_2_ = bf16[512,512]{1,0:T(8,128)(2,1)S(1)} collective-permute-done((bf16[512,512]{1,0:T(8,128)(2,1)S(1)}, bf16[512,512]{1,0:T(8,128)(2,1)S(1)}, u32[]{:S(2)}, u32[]{:S(2)}) %collective-permute-start.1) | collective-permute-done | bytes 524320 | tf_op jit(solution)/shard_map/ppermute | solution.py:180
  66.5 1.0 broadcast_select_fusion.3
  67.4 0.4 collective-permute-start.3
  67.8 0.1 copy.12
  67.9 0.1 reduce
  68.1 0.0 collective-permute-done.6.refs_2_
  68.1 0.1 broadcast_select_fusion.2
  68.2 1.7 collective-permute-start.8
  69.9 0.1 add_bitcast_fusion
  70.0 0.0 collective-permute-start.2
  70.0 17.4 %collective-permute-done.3.refs_4_ = bf16[512,512]{1,0:T(8,128)(2,1)} collective-permute-done((bf16[512,512]{1,0:T(8,128)(2,1)}, bf16[512,512]{1,0:T(8,128)(2,1)}, u32[]{:S(2)}, u32[]{:S(2)}) %collective-permute-start.3) | collective-permute-done | bytes 524320 | tf_op jit(solution)/shard_map/ppermute | solution.py:180
  87.4 0.0 collective-permute-start.4
  87.4 0.1 select_reduce_fusion
  87.5 0.8 iota_subtract_fusion.low_minus_lane
  88.3 0.0 collective-permute-done.refs_1_
  88.3 0.5 collective-permute-start.7
  88.8 15.3 %collective-permute-done.8.refs_4_ = bf16[512,512]{1,0:T(8,128)(2,1)S(1)} collective-permute-done((bf16[512,512]{1,0:T(8,128)(2,1)S(1)}, bf16[512,512]{1,0:T(8,128)(2,1)S(1)}, u32[]{:S(2)}, u32[]{:S(2)}) %collective-permute-start.8) | collective-permute-done | bytes 524320 | tf_op jit(solution)/shard_map/ppermute | solution.py:180
  104.1 0.0 collective-permute-start.9
  104.1 0.2 select_reduce_fusion.2
  104.4 0.1 select_n.67
  104.4 0.6 pad_add_fusion.table
  105.0 0.0 collective-permute-done.2.refs_3_
  105.0 0.0 collective-permute-done.4.refs_5_
  105.1 17.7 %attend.2 = bf16[512,1024]{1,0:T(8,128)(2,1)} custom-call(s32[36]{0:T(128)} %pad_add_fusion.table, bf16[512,2048]{1,0:T(8,128)(2,1)} %queries.3, s32[512,128]{1,0:T(8,128)} %iota_subtract_fusion.low_minus_lane, bf16[512,512]{1,0:T(8,128)(2,1)} %copy-done.4, bf16[512,512]{1,0:T(8,128)(2,1)} %collective-permute-done.refs_1_, bf16[512,512]{1,0:T(8,128)(2,1)} %copy-done.5, ...), custom_call_target="tpu_custom_call" | custom-call | flops 4294967296 | bytes 6291456 | tf_op jit(solution)/shard_map/attend/pallas_call | solution.py:148
  122.8 0.3 collective-permute-start.10
  123.1 0.0 collective-permute-done.5.refs_1_
  123.1 0.0 collective-permute-done.7.refs_3_
  123.1 0.0 collective-permute-done.9.refs_5_
  123.1 17.7 %attend.3 = bf16[512,1024]{1,0:T(8,128)(2,1)} custom-call(s32[36]{0:T(128)} %pad_add_fusion.table, bf16[512,2048]{1,0:T(8,128)(2,1)} %queries.3, s32[512,128]{1,0:T(8,128)} %iota_subtract_fusion.low_minus_lane, bf16[512,512]{1,0:T(8,128)(2,1)} %copy-done.2, bf16[512,512]{1,0:T(8,128)(2,1)} %collective-permute-done.5.refs_1_, bf16[512,512]{1,0:T(8,128)(2,1)} %copy-done.3, ...), custom_call_target="tpu_custom_call" | custom-call | flops 4294967296 | bytes 6291456 | tf_op jit(solution)/shard_map/attend/pallas_call | solution.py:148
  140.8 1.9 collective-permute-start.11
  142.6 6.4 %collective-permute-done.10 = bf16[512,1024]{1,0:T(8,128)(2,1)S(1)} collective-permute-done((bf16[512,1024]{1,0:T(8,128)(2,1)}, bf16[512,1024]{1,0:T(8,128)(2,1)S(1)}, u32[]{:S(2)}, u32[]{:S(2)}) %collective-permute-start.10) | collective-permute-done | bytes 1048608 | tf_op jit(solution)/shard_map/ppermute | solution.py:180
  149.1 0.1 constant_dynamic-update-slice_fusion.1
  149.2 16.6 %collective-permute-done.11 = bf16[512,1024]{1,0:T(8,128)(2,1)S(1)} collective-permute-done((bf16[512,1024]{1,0:T(8,128)(2,1)}, bf16[512,1024]{1,0:T(8,128)(2,1)S(1)}, u32[]{:S(2)}, u32[]{:S(2)}) %collective-permute-start.11) | collective-permute-done | bytes 1048608 | tf_op jit(solution)/shard_map/ppermute | solution.py:180
  165.8 0.1 constant_dynamic-update-slice_fusion
  165.9 2.3 %broadcast_select_fusion.1 = (bf16[512,2048]{1,0:T(8,128)(2,1)S(1)}, bf16[512,2048]{1,0:T(8,128)(2,1)}) fusion(bf16[512,2048]{1,0:T(8,128)(2,1)S(1)} %constant_dynamic-update-slice_fusion, pred[]{:T(512)S(6)} %eq.9, bf16[512,1024]{1,0:T(8,128)(2,1)S(1)} %copy-done.1, bf16[512,1024]{1,0:T(8,128)(2,1)S(1)} %copy-done), kind=kLoop, calls=%fused_computation.8 | loop fusion | flops 6291456 | bytes 8388609 | tf_op jit(solution)/shard_map/jit(_where)/select_n | solution.py:234
  168.2 13.9 %fusion.4 = bf16[512,2048]{1,0:T(8,128)(2,1)} fusion(bf16[4096,2048]{1,0:T(8,128)(2,1)} %all-gather.2.cloned.1.call-done, bf16[512,2048]{1,0:T(8,128)(2,1)} %get-tuple-element.8, bf16[512,2048]{1,0:T(8,128)(2,1)S(1)} %get-tuple-element.7), kind=kOutput, calls=%fused_computation.5 | convolution fusion | flops 8599371776 | bytes 23068672 | tf_op jit(solution)/shard_map/dot_general | solution.py:237
  (29 shorter events, 0.2 us)
Async XLA Ops:
  6.5 161.7 %all-gather.2.cloned.1.call-start = ((), (), s32[]{:S(2)}) async-start(), calls=%async_computation | async-start | bytes 17825792 | tf_op jit(solution)/shard_map/all_gather | solution.py:230
  7.3 4.6 %copy-start.6 = (s32[16,4]{0,1:T(4,128)S(1)}, s32[16,4]{0,1:T(4,128)}, u32[]{:S(2)}) copy-start(s32[16,4]{0,1:T(4,128)} %param.9) | copy-start | bytes 772
  8.5 59.3 %copy-start.7 = (s32[16]{0:T(128)S(1)}, s32[16]{0:T(128)}, u32[]{:S(2)}) copy-start(s32[16]{0:T(128)} %param.10) | copy-start | bytes 196
  8.6 59.6 %copy-start.2 = (bf16[512,512]{1,0:T(8,128)(2,1)}, bf16[512,512]{1,0:T(8,128)(2,1)S(1)}, u32[]{:S(2)}) copy-start(bf16[512,512]{1,0:T(8,128)(2,1)S(1)} %pad_maximum_fusion.2.refs_0_) | copy-start | bytes 1572868
  8.6 59.5 %collective-permute-start.6 = (bf16[512,512]{1,0:T(8,128)(2,1)S(1)}, bf16[512,512]{1,0:T(8,128)(2,1)S(1)}, u32[]{:S(2)}, u32[]{:S(2)}) collective-permute-start(bf16[512,512]{1,0:T(8,128)(2,1)S(1)} %pad_maximum_fusion.2.refs_0_), channel_id=1, source_target_pairs={{0,8},{2,10},{4,12},{6,14},{8,16},{10,18},{12,20},{14,22},{16,24},... | collective-permute-start | bytes 1572872 | tf_op jit(solution)/shard_map/ppermute | solution.py:180
  9.9 113.2 %collective-permute-start.5 = (bf16[512,512]{1,0:T(8,128)(2,1)S(1)}, bf16[512,512]{1,0:T(8,128)(2,1)}, u32[]{:S(2)}, u32[]{:S(2)}) collective-permute-start(bf16[512,512]{1,0:T(8,128)(2,1)S(1)} %pad_maximum_fusion.2.refs_0_), channel_id=1, source_target_pairs={{0,2},{2,0},{4,6},{6,4},{8,10},{10,8},{12,14},{14,12},{16,18},{18,... | collective-permute-start | bytes 1572872 | tf_op jit(solution)/shard_map/ppermute | solution.py:180
  10.0 95.0 %copy-start.4 = (bf16[512,512]{1,0:T(8,128)(2,1)}, bf16[512,512]{1,0:T(8,128)(2,1)S(1)}, u32[]{:S(2)}) copy-start(bf16[512,512]{1,0:T(8,128)(2,1)S(1)} %pad_maximum_fusion.1.refs_0_) | copy-start | bytes 1572868
  10.0 56.4 %collective-permute-start.1 = (bf16[512,512]{1,0:T(8,128)(2,1)S(1)}, bf16[512,512]{1,0:T(8,128)(2,1)S(1)}, u32[]{:S(2)}, u32[]{:S(2)}) collective-permute-start(bf16[512,512]{1,0:T(8,128)(2,1)S(1)} %pad_maximum_fusion.1.refs_0_), channel_id=1, source_target_pairs={{0,8},{2,10},{4,12},{6,14},{8,16},{10,18},{12,20},{14,22},{16,24},... | collective-permute-start | bytes 1572872 | tf_op jit(solution)/shard_map/ppermute | solution.py:180
  11.3 77.0 %collective-permute-start = (bf16[512,512]{1,0:T(8,128)(2,1)S(1)}, bf16[512,512]{1,0:T(8,128)(2,1)}, u32[]{:S(2)}, u32[]{:S(2)}) collective-permute-start(bf16[512,512]{1,0:T(8,128)(2,1)S(1)} %pad_maximum_fusion.1.refs_0_), channel_id=1, source_target_pairs={{0,2},{2,0},{4,6},{6,4},{8,10},{10,8},{12,14},{14,12},{16,18},{18,... | collective-permute-start | bytes 1572872 | tf_op jit(solution)/shard_map/ppermute | solution.py:180
  66.5 38.6 %copy-start.5 = (bf16[512,512]{1,0:T(8,128)(2,1)}, bf16[512,512]{1,0:T(8,128)(2,1)S(1)}, u32[]{:S(2)}) copy-start(bf16[512,512]{1,0:T(8,128)(2,1)S(1)} %collective-permute-done.1.refs_2_) | copy-start | bytes 1572868
  67.4 20.0 %collective-permute-start.3 = (bf16[512,512]{1,0:T(8,128)(2,1)}, bf16[512,512]{1,0:T(8,128)(2,1)}, u32[]{:S(2)}, u32[]{:S(2)}) collective-permute-start(bf16[512,512]{1,0:T(8,128)(2,1)} %broadcast_select_fusion.3), channel_id=1, source_target_pairs={{0,4},{2,6},{4,0},{6,2},{8,12},{10,14},{12,8},{14,10},{16,20},{18,... | collective-permute-start | bytes 1572872 | tf_op jit(solution)/shard_map/ppermute | solution.py:180
  68.1 54.7 %copy-start.3 = (bf16[512,512]{1,0:T(8,128)(2,1)}, bf16[512,512]{1,0:T(8,128)(2,1)S(1)}, u32[]{:S(2)}) copy-start(bf16[512,512]{1,0:T(8,128)(2,1)S(1)} %collective-permute-done.6.refs_2_) | copy-start | bytes 1572868
  68.2 35.9 %collective-permute-start.8 = (bf16[512,512]{1,0:T(8,128)(2,1)S(1)}, bf16[512,512]{1,0:T(8,128)(2,1)S(1)}, u32[]{:S(2)}, u32[]{:S(2)}) collective-permute-start(bf16[512,512]{1,0:T(8,128)(2,1)S(1)} %broadcast_select_fusion.2), channel_id=1, source_target_pairs={{0,4},{2,6},{4,0},{6,2},{8,12},{10,14},{12,8},{14,10},{16,20},{18,... | collective-permute-start | bytes 1572872 | tf_op jit(solution)/shard_map/ppermute | solution.py:180
  70.0 35.0 %collective-permute-start.2 = (bf16[512,512]{1,0:T(8,128)(2,1)S(1)}, bf16[512,512]{1,0:T(8,128)(2,1)}, u32[]{:S(2)}, u32[]{:S(2)}) collective-permute-start(bf16[512,512]{1,0:T(8,128)(2,1)S(1)} %collective-permute-done.1.refs_2_), channel_id=1, source_target_pairs={{0,2},{2,0},{4,6},{6,4},{8,10},{10,8},{12,14},{14,12},{16,18},{18,... | collective-permute-start | bytes 1572872 | tf_op jit(solution)/shard_map/ppermute | solution.py:180
  87.4 17.7 %collective-permute-start.4 = (bf16[512,512]{1,0:T(8,128)(2,1)}, bf16[512,512]{1,0:T(8,128)(2,1)}, u32[]{:S(2)}, u32[]{:S(2)}) collective-permute-start(bf16[512,512]{1,0:T(8,128)(2,1)} %collective-permute-done.3.refs_4_), channel_id=1, source_target_pairs={{0,2},{2,0},{4,6},{6,4},{8,10},{10,8},{12,14},{14,12},{16,18},{18,... | collective-permute-start | bytes 1572872 | tf_op jit(solution)/shard_map/ppermute | solution.py:180
  88.3 34.8 %collective-permute-start.7 = (bf16[512,512]{1,0:T(8,128)(2,1)S(1)}, bf16[512,512]{1,0:T(8,128)(2,1)}, u32[]{:S(2)}, u32[]{:S(2)}) collective-permute-start(bf16[512,512]{1,0:T(8,128)(2,1)S(1)} %collective-permute-done.6.refs_2_), channel_id=1, source_target_pairs={{0,2},{2,0},{4,6},{6,4},{8,10},{10,8},{12,14},{14,12},{16,18},{18,... | collective-permute-start | bytes 1572872 | tf_op jit(solution)/shard_map/ppermute | solution.py:180
  104.1 18.6 %copy-start.8 = (bf16[512,512]{1,0:T(8,128)(2,1)}, bf16[512,512]{1,0:T(8,128)(2,1)S(1)}, u32[]{:S(2)}) copy-start(bf16[512,512]{1,0:T(8,128)(2,1)S(1)} %collective-permute-done.8.refs_4_) | copy-start | bytes 1572868
  104.1 18.9 %collective-permute-start.9 = (bf16[512,512]{1,0:T(8,128)(2,1)S(1)}, bf16[512,512]{1,0:T(8,128)(2,1)}, u32[]{:S(2)}, u32[]{:S(2)}) collective-permute-start(bf16[512,512]{1,0:T(8,128)(2,1)S(1)} %collective-permute-done.8.refs_4_), channel_id=1, source_target_pairs={{0,2},{2,0},{4,6},{6,4},{8,10},{10,8},{12,14},{14,12},{16,18},{18,... | collective-permute-start | bytes 1572872 | tf_op jit(solution)/shard_map/ppermute | solution.py:180
  122.8 26.3 %collective-permute-start.10 = (bf16[512,1024]{1,0:T(8,128)(2,1)}, bf16[512,1024]{1,0:T(8,128)(2,1)S(1)}, u32[]{:S(2)}, u32[]{:S(2)}) collective-permute-start(bf16[512,1024]{1,0:T(8,128)(2,1)} %attend.2), channel_id=1, source_target_pairs={{0,1},{1,0},{2,3},{3,2},{4,5},{5,4},{6,7},{7,6},{8,9},{9,8},{10,11... | collective-permute-start | bytes 3145736 | tf_op jit(solution)/shard_map/ppermute | solution.py:180
  140.8 25.0 %collective-permute-start.11 = (bf16[512,1024]{1,0:T(8,128)(2,1)}, bf16[512,1024]{1,0:T(8,128)(2,1)S(1)}, u32[]{:S(2)}, u32[]{:S(2)}) collective-permute-start(bf16[512,1024]{1,0:T(8,128)(2,1)} %attend.3), channel_id=1, source_target_pairs={{0,1},{1,0},{2,3},{3,2},{4,5},{5,4},{6,7},{7,6},{8,9},{9,8},{10,11... | collective-permute-start | bytes 3145736 | tf_op jit(solution)/shard_map/ppermute | solution.py:180
  142.6 23.2 %copy-start = (bf16[512,1024]{1,0:T(8,128)(2,1)S(1)}, bf16[512,1024]{1,0:T(8,128)(2,1)}, u32[]{:S(2)}) copy-start(bf16[512,1024]{1,0:T(8,128)(2,1)} %attend.2) | copy-start | bytes 3145732
  142.6 23.2 %copy-start.1 = (bf16[512,1024]{1,0:T(8,128)(2,1)S(1)}, bf16[512,1024]{1,0:T(8,128)(2,1)}, u32[]{:S(2)}) copy-start(bf16[512,1024]{1,0:T(8,128)(2,1)} %attend.3) | copy-start | bytes 3145732
Sparse Core Ops, SparseCore 0:
  9.5 147.2 all-gather.1
